TPU v7x, 32 devices: a whole 2x2x4 slice. The times are simulated.
32 devices in a mesh: gx: 4 (over y, x), gy: 4 (over z), gz: 2 (over core).
Axes of the slice: x: 2, y: 2, z: 4, core: 2. Of those that a mesh axis runs over, the one named last changes fastest.
Arguments:
- charges: float32 [128, 256, 256], P('gx', 'gy', 'gz'), may hold values from -8 to 8
- kernel_taps: float32 [5, 3, 17], replicated, may hold values from 0.08 to 0.4
Outputs:
- potential: float32 [128, 256, 256], P('gx', 'gy', 'gz')
All inputs are finite; a program needn't handle non-finite values.
Results may differ from a plain program's by a relative error of at most 0.00029.
Values sent between devices are 32-bit elements; how exact they have to be, the bound alone decides.
A program may use at most 128 MiB of HBM per device.

v0:
```python
import functools

import jax
import jax.numpy as jnp
from jax import lax
from jax.experimental import pallas as pl
from jax.experimental.pallas import tpu as pltpu
from jax.sharding import PartitionSpec as P

F32, BF16 = jnp.float32, jnp.bfloat16
LANES = 128
AXES = ("gx", "gy", "gz")
ODD = (-0.0625, 0.5625, 0.5625, -0.0625)
SIDES = tuple((a, b) for a in (-1, 0, 1) for b in (-1, 0, 1) if (a, b) != (0, 0))


def split(v):
    hi = v.astype(BF16)
    return hi, (v - hi.astype(F32)).astype(BF16)


def mm(a, b):
    return jnp.dot(a, b, preferred_element_type=F32)


def exact(a, b):
    return jnp.dot(a, b, preferred_element_type=F32, precision=lax.Precision.HIGHEST)


def dot_right(v, w):
    hi, lo = split(v)
    out = mm(hi, w[0][...]) + mm(lo, w[0][...])
    return out if w[1] is None else out + mm(hi, w[1][...])


def dot_left(w_ref, v, terms):
    hi, lo = split(v)
    return mm(w_ref[...], jnp.concatenate([hi, lo, hi][:terms], axis=0))


def grids(rows, cols):
    return (
        lax.broadcasted_iota(jnp.int32, (rows, cols), 0),
        lax.broadcasted_iota(jnp.int32, (rows, cols), 1),
    )


def pick(taps, level, axis, diff, ok):
    out = jnp.zeros(diff.shape, F32)
    for t in range(17):
        out = jnp.where(diff == t, taps[level, axis, t], out)
    return jnp.where(ok, out, 0.0)


def cubic(diff, ok):
    d = jnp.abs(diff)
    out = jnp.where(d == 0, 1.0, jnp.where(d == 1, 0.5625, jnp.where(d == 3, -0.0625, 0.0)))
    return jnp.where(ok, out, 0.0).astype(F32)


def up(n, m):
    return -(-n // m) * m


def inside(v, n):
    return (v >= 0) & (v < n)


def kernel(counts, dims, taps, x_ref, out_ref, e0, l0, r0, y0, y1, e1, l1, r1, t1, s1, g2, u2, y2, p2, d1,
           w0h, w0l, m0, w1h, w1l, m1, w2h, w2l, m2, c2, pz2, py2, pz1, py1,
           sa, ra, sza, rza, sb, rb, szb, rzb, sg, rg):
    nx, ny, nz = counts
    bx, by, bz = dims
    here = tuple(lax.axis_index(a) for a in AXES)
    gx, gy, gz = here
    cx, cy, cz = bx // 2, by // 2, bz // 2
    fx, fy, fz = bx // 4, by // 4, bz // 4

    def there(dx, dy, dz):
        return inside(gx + dx, nx) & inside(gy + dy, ny) & inside(gz + dz, nz)

    partners = [(a, b, 0) for a, b in SIDES] + [(0, 0, -1), (0, 0, 1)]
    for dim, n in enumerate(counts):
        for d in range(2, n):
            for sgn in (-d, d):
                partners.append(tuple(sgn if k == dim else 0 for k in range(3)))
    barrier = pltpu.get_barrier_semaphore()
    total = jnp.int32(0)
    for p in partners:
        ok = there(*p)
        total = total + ok.astype(jnp.int32)

        @pl.when(ok)
        def _(p=p):
            pl.semaphore_signal(
                barrier, inc=1, device_id=(gx + p[0], gy + p[1], gz + p[2]),
                device_id_type=pl.DeviceIdType.MESH,
            )

    def zero_halo(ref, wx, wy, mx, my):
        for a, b in SIDES:
            @pl.when(jnp.logical_not(there(a, b, 0)))
            def _(a=a, b=b):
                xs = {-1: (0, wx), 0: (wx, mx), 1: (wx + mx, wx)}[a]
                ys = {-1: (0, wy), 0: (wy, my), 1: (wy + my, wy)}[b]
                ref[pl.ds(*xs), pl.ds(*ys), :] = jnp.zeros((xs[1], ys[1], LANES), F32)

    zero_halo(e0, 8, 8, bx, by)
    zero_halo(e1, 5, 16, cx // 2, cy)
    pl.semaphore_wait(barrier, total)

    def exchange(src, base, ref, wx, wy, mx, my, send, recv):
        out = []
        for k, (a, b) in enumerate(SIDES):
            sx = {-1: (0, wx), 0: (0, mx), 1: (mx - wx, wx)}[a]
            sy = {-1: (0, wy), 0: (0, my), 1: (my - wy, wy)}[b]
            tx = {-1: (wx + mx, wx), 0: (wx, mx), 1: (0, wx)}[a]
            ty = {-1: (wy + my, wy), 0: (wy, my), 1: (0, wy)}[b]
            copy = pltpu.make_async_remote_copy(
                src_ref=src.at[pl.ds(base[0] + sx[0], sx[1]), pl.ds(base[1] + sy[0], sy[1]), :],
                dst_ref=ref.at[pl.ds(*tx), pl.ds(*ty), :],
                send_sem=send.at[k], recv_sem=recv.at[k],
                device_id=(gx + a, gy + b, gz), device_id_type=pl.DeviceIdType.MESH,
            )
            out.append((there(a, b, 0), there(-a, -b, 0), copy))
        return out

    def across(src, base, left, right, ranges, send, recv):
        out = []
        for k, (ofs, xs, ys) in enumerate(ranges):
            for h, (dz, dst) in enumerate(((1, left), (-1, right))):
                source = (src if k == 0 else base)
                copy = pltpu.make_async_remote_copy(
                    src_ref=source.at[pl.ds(xs[0] - ofs[0], xs[1]), pl.ds(ys[0] - ofs[1], ys[1]), :],
                    dst_ref=dst.at[pl.ds(*xs), pl.ds(*ys), :],
                    send_sem=send.at[k, h], recv_sem=recv.at[k, h],
                    device_id=(gx, gy, gz + dz), device_id_type=pl.DeviceIdType.MESH,
                )
                out.append((there(0, 0, dz), there(0, 0, -dz), copy))
        return out

    def start(copies):
        for to, _, copy in copies:
            pl.when(to)(copy.start)

    def arrive(copies):
        for _, fro, copy in copies:
            pl.when(fro)(copy.wait_recv)

    def left_over(copies):
        for to, _, copy in copies:
            pl.when(to)(copy.wait_send)

    def pieces(wx, wy, mx, my, direct):
        o = (wx, wy) if direct else (0, 0)
        n = (0, 0)
        return [
            (o, (wx, mx), (wy, my)),
            (n, (0, wx), (0, my + 2 * wy)),
            (n, (wx + mx, wx), (0, my + 2 * wy)),
            (n, (wx, mx), (0, wy)),
            (n, (wx, mx), (wy + my, wy)),
        ]

    xa = exchange(x_ref, (0, 0), e0, 8, 8, bx, by, sa, ra)
    za = across(x_ref, e0, l0, r0, pieces(8, 8, bx, by, True), sza, rza)
    start(xa)
    start(za[:2])
    e0[pl.ds(8, bx), pl.ds(8, by), :] = x_ref[...]

    def put(h, l, v):
        hi, lo = split(v)
        h[...] = hi
        if l is not None:
            l[...] = lo

    def stack(ref, v, terms):
        hi, lo = split(v)
        ref[...] = jnp.concatenate([hi, hi, lo][:terms], axis=1)

    i, j = grids(2 * bz, bz)
    pos = jnp.where(i < bz + bz // 2, i, i - 2 * bz)
    k0 = pick(taps, 0, 2, pos - j + 8, inside(pos, bz + 8) | inside(pos + 8, 8))
    rz = cubic(pos - 2 * j, j < cz)
    put(w0h, w0l, jnp.concatenate([k0, rz], axis=1))
    i, j = grids(by + cy, by + 16)
    stack(m0, jnp.where(i < by, pick(taps, 0, 1, j - i, i < by), cubic(j - 8 - 2 * (i - by), i >= by)), 3)
    i, j = grids(2 * cz, LANES)
    pos = jnp.where(i < cz + cz // 2, i, i - 2 * cz)
    kk = j - 2
    top = cz + 4
    ok = (j < top) & inside(gz * cz + kk, nz * cz)
    rlane = LANES - fz
    put(w1h, w1l, pick(taps, 1, 2, pos - kk + 8, ok) + cubic(pos - 2 * (j - rlane), j >= rlane))
    ry1 = up(cy + 4, 8)
    i, j = grids(ry1 + fy, cy + 32)
    ok = (i < cy + 4) & inside(gy * cy + i - 2, ny * cy)
    stack(m1, pick(taps, 1, 1, j - 16 - (i - 2) + 8, ok) + cubic(j - 16 - 2 * (i - ry1), i >= ry1), 3)
    def plain(axis, level, n, pad, turned):
        i, j = grids(pad, pad)
        d = (i - j if turned else j - i) + 8
        return pick(taps, level, axis, d, (i < n) & (j < n))

    def rest(n, pad, big, turned_r):
        i, j = grids(*((big, pad) if turned_r else (pad, big)))
        c, f = (j, i) if turned_r else (i, j)
        return cubic(f - 2 * c, (c < n) & (f < 2 * n))

    def operators(axis, n2, first, rows, count):
        n3, n4 = n2 // 2, n2 // 4
        q = up(n2, LANES)
        i, j = grids(rows, q)
        g = first + i
        ok = (i < count) & inside(g, n2)
        one = pick(taps, 2, axis, j - g + 8, ok & (j < n2))
        pr = cubic(g - 2 * j, ok & (j < n3))
        r23, r34 = rest(n3, q, q, False), rest(n4, q, q, False)
        p34 = rest(n4, q, q, True)
        two = exact(exact(pr, plain(axis, 3, n3, q, False)), r23)
        three = exact(exact(exact(exact(pr, p34), plain(axis, 4, n4, q, False)), r34), r23)
        return one, two, three

    n2x, n2y, n2z = nx * fx, ny * fy, nz * fz
    ez, ey, ex = fz + 5, fy + 5, fx + 5
    tz = 40
    row = lax.broadcasted_iota(jnp.int32, (LANES, 1), 0)
    ops = operators(2, n2z, gz * fz - 2, tz, ez)
    cols = jnp.concatenate(list(ops) + [jnp.zeros((LANES - 3 * tz, ops[0].shape[1]), F32)], axis=0)
    put(w2h, w2l, cols.T)
    ty = up(ey, 8)
    ops = operators(1, n2y, gy * fy - 2, ty, ey)
    stack(m2, jnp.concatenate(list(ops), axis=0)[:, :n2y], 3)
    tx = up(ex, 8)
    ops = operators(0, n2x, gx * fx - 2, tx, ex)
    lane = lax.broadcasted_iota(jnp.int32, (1, LANES), 1)
    tall = [o.T for o in ops]
    for r in range(ex):
        a, b, c = (o[:n2x, r:r + 1] for o in tall)
        c2[r] = jnp.where(lane < tz, a, jnp.where(lane < 2 * tz, b, c))
    i, j = grids(LANES, LANES)
    src = i - jnp.where(i < tz, 0, jnp.where(i < 2 * tz, tz, 2 * tz)) - 2
    put(pz2, None, cubic((j - 2) - 2 * src, (i < 3 * tz) & (src < fz + 3) & (j < top) & inside(gz * cz + j - 2, nz * cz)))
    i, j = grids(ry1, up(ty, 16))
    stack(py2, cubic((i - 2) - 2 * (j - 2), (j < ey) & (i < cy + 4) & inside(gy * cy + i - 2, ny * cy)), 2)
    i, j = grids(LANES, bz)
    put(pz1, None, cubic(j - 2 * (i - 2), i < top))
    i, j = grids(by, up(ry1, 16))
    stack(py1, cubic(i - 2 * (j - 2), j < cy + 4), 2)

    arrive(xa)
    start(za[2:])
    arrive(za)

    wide = by + 16
    has_r, has_l = there(0, 0, 1), there(0, 0, -1)
    mask_r, mask_l = (lane < LANES // 2) & has_r, (lane >= LANES // 2) & has_l
    step0 = 4

    @pl.loop(0, (bx + 16) // step0)
    def _(c):
        at = pl.ds(c * step0, step0)
        own = e0[at].reshape(step0 * wide, LANES)
        other = jnp.where(
            mask_r, r0[at].reshape(step0 * wide, LANES),
            jnp.where(mask_l, l0[at].reshape(step0 * wide, LANES), 0.0),
        )
        v = dot_right(jnp.concatenate([own, other], axis=1), (w0h, w0l))
        for k in range(step0):
            o = dot_left(m0, v[k * wide:(k + 1) * wide], 3)
            y0[c * step0 + k] = o[:by, :LANES]
            y1[c * step0 + k] = o[by:, LANES:]

    def restrict_x(ref, at):
        return (
            ref[at] + 0.5625 * (ref[at - 1] + ref[at + 1]) - 0.0625 * (ref[at - 3] + ref[at + 3])
        )

    @pl.loop(0, cx // 2)
    def _(p):
        a = restrict_x(y1, 8 + 4 * p)
        b = restrict_x(y1, 10 + 4 * p)
        t1[p] = jnp.where(lane < cz, a, pltpu.roll(b, cz, 1))

    own_copy = pltpu.make_async_copy(t1, e1.at[pl.ds(5, cx // 2), pl.ds(16, cy), :], sg.at[3, 0])
    own_copy.start()
    own_copy.wait()
    xb = exchange(e1, (5, 16), e1, 5, 16, cx // 2, cy, sb, rb)
    zb = across(e1, e1, l1, r1, pieces(5, 16, cx // 2, cy, False), szb, rzb)
    start(xb)
    start(zb[:2])

    @pl.loop(0, bx)
    def _(p):
        acc = taps[0, 0, 0] * y0[p]
        for t in range(1, 17):
            acc = acc + taps[0, 0, t] * y0[p + t]
        out_ref[p] = acc

    arrive(xb)
    start(zb[2:])
    arrive(zb)

    half = lax.rem(lane, cz) < cz // 2

    @pl.loop(0, cx // 2 + 10)
    def _(p):
        own = e1[p]
        other = jnp.where(half & has_r, r1[p], jnp.where(jnp.logical_not(half) & has_l, l1[p], 0.0))
        even = jnp.where(lane < cz, own, pltpu.roll(other, cz, 1))
        odd = jnp.where(lane < cz, pltpu.roll(own, cz, 1), other)
        h = own.shape[0]
        v = dot_right(jnp.concatenate([even, odd], axis=0), (w1h, w1l))
        o = dot_left(m1, jnp.concatenate([v[:h], v[h:]], axis=1), 3)
        s1[2 * p] = o[:, :LANES]
        s1[2 * p + 1] = o[:, LANES:]

    per = LANES // fz
    def restrict_1(q):
        at = 10 + 2 * q
        rows = pl.ds(ry1, fy)
        v = (
            s1[at, rows] + 0.5625 * (s1[at - 1, rows] + s1[at + 1, rows])
            - 0.0625 * (s1[at - 3, rows] + s1[at + 3, rows])
        )
        return jnp.where(lane >= rlane, v, 0.0)

    np2 = fx // per
    for p in range(np2):
        acc = None
        for k in range(per):
            v = restrict_1(p * per + k)
            sh = (fz * k + LANES - rlane) % LANES
            v = pltpu.roll(v, sh, 1) if sh else v
            acc = v if acc is None else acc + v
        p2[p] = acc
    own_copy = pltpu.make_async_copy(p2, g2.at[gz, gy, pl.ds(gx * np2, np2)], sg.at[3, 1])
    own_copy.start()
    own_copy.wait()

    def spread(dim, n, ref, k0):
        out = []
        for m, d in enumerate([d for d in range(-(n - 1), n) if d]):
            dev = tuple(here[k] + (d if k == dim else 0) for k in range(3))
            copy = pltpu.make_async_remote_copy(
                src_ref=ref(here[dim]), dst_ref=ref(here[dim]),
                send_sem=sg.at[dim, m], recv_sem=rg.at[dim, m],
                device_id=dev, device_id_type=pl.DeviceIdType.MESH,
            )
            land = pltpu.make_async_remote_copy(
                src_ref=ref(here[dim]), dst_ref=ref(here[dim] - d),
                send_sem=sg.at[dim, m], recv_sem=rg.at[dim, m],
                device_id=dev, device_id_type=pl.DeviceIdType.MESH,
            )
            to = inside(here[dim] + d, n)
            fro = inside(here[dim] - d, n)
            out.append((to, fro, copy, land))
        return out

    def begin(copies):
        for to, _, copy, _ in copies:
            pl.when(to)(copy.start)

    def landed(copies):
        for _, fro, _, land in copies:
            pl.when(fro)(land.wait_recv)

    ca = spread(0, nx, lambda k: g2.at[gz, gy, pl.ds(k * np2, np2)], 0)
    begin(ca)
    seen = lambda r: inside(gx * cx + r - 2, nx * cx).astype(F32)

    @pl.loop(0, cx + 4)
    def _(p):
        rows = pl.ds(0, ry1)
        acc = taps[1, 0, 0] * s1[p, rows]
        for t in range(1, 17):
            acc = acc + taps[1, 0, t] * s1[p + t, rows]
        d1[p] = acc
    landed(ca)
    cb = spread(1, ny, lambda k: g2.at[gz, k], 0)
    begin(cb)
    landed(cb)
    cc = spread(2, nz, lambda k: g2.at[k], 0)
    begin(cc)
    landed(cc)

    tiles = u2.shape[0]

    @pl.loop(0, nx * np2)
    def _(p):
        for b in range(ny):
            for k in range(per):
                for t in range(tiles):
                    acc = jnp.zeros((fy, LANES), F32)
                    for s in range(t * per, min(nz, (t + 1) * per)):
                        v = g2[s, b, p]
                        sh = (fz * (s - t * per - k)) % LANES
                        v = pltpu.roll(v, sh, 1) if sh else v
                        lo = fz * (s - t * per)
                        acc = jnp.where((lane >= lo) & (lane < lo + fz), v, acc)
                    u2[t, p * per + k, pl.ds(b * fy, fy), :] = acc

    step2 = 2

    @pl.loop(0, n2x // step2)
    def _(c):
        at = pl.ds(c * step2, step2)
        v = jnp.concatenate([u2[t, at].reshape(step2 * n2y, LANES) for t in range(tiles)], axis=1)
        v = dot_right(v, (w2h, w2l))
        v = jnp.concatenate([v[k * n2y:(k + 1) * n2y] for k in range(step2)], axis=1)
        o = dot_left(m2, v, 3)
        for k in range(step2):
            w = o[:, k * LANES:(k + 1) * LANES]
            y2[c * step2 + k] = jnp.where(
                lane < tz, w[:ty], jnp.where(lane < 2 * tz, w[ty:2 * ty], w[2 * ty:])
            )

    parts = []
    for r in range(ex):
        acc = c2[r, pl.ds(0, 1)] * y2[0]
        for q in range(1, n2x):
            acc = acc + c2[r, pl.ds(q, 1)] * y2[q]
        parts.append(acc)
    v = dot_right(jnp.concatenate(parts, axis=0), (pz2, None))
    fill = up(ty, 16) - ty
    pro = []
    for r in range(ex):
        w = v[r * ty:(r + 1) * ty]
        if fill:
            w = jnp.concatenate([w, jnp.zeros((fill, LANES), F32)], axis=0)
        pro.append(dot_left(py2, w, 2))
    for p in range(cx + 4):
        m = (p - 2) // 2 + 2
        if p % 2 == 0:
            w = pro[m]
        else:
            w = 0.5625 * (pro[m] + pro[m + 1]) - 0.0625 * (pro[m - 1] + pro[m + 2])
        d1[p] = (d1[p] + w) * seen(p)

    fill1 = up(ry1, 16) - ry1

    @pl.loop(0, (cx + 4) // 2)
    def _(c):
        v = dot_right(d1[pl.ds(2 * c, 2)].reshape(2 * ry1, LANES), (pz1, None))
        v = jnp.concatenate([v[:ry1], v[ry1:]], axis=1)
        if fill1:
            v = jnp.concatenate([v, jnp.zeros((fill1, 2 * LANES), F32)], axis=0)
        o = dot_left(py1, v, 2)
        y0[2 * c] = o[:, :LANES]
        y0[2 * c + 1] = o[:, LANES:]

    @pl.loop(0, cx)
    def _(m):
        at = m + 2
        out_ref[2 * m] = out_ref[2 * m] + y0[at]
        out_ref[2 * m + 1] = out_ref[2 * m + 1] + (
            0.5625 * (y0[at] + y0[at + 1]) - 0.0625 * (y0[at - 1] + y0[at + 2])
        )

    for group in (xa, za, xb, zb):
        left_over(group)
    for group in (ca, cb, cc):
        for to, _, copy, _ in group:
            pl.when(to)(copy.wait_send)


def per_device(counts, charges, kernel_taps):
    nx, ny, nz = counts
    bx, by, bz = dims = charges.shape
    assert bz == LANES
    cx, cy, cz = bx // 2, by // 2, bz // 2
    fx, fy, fz = bx // 4, by // 4, bz // 4
    n2x, n2y, n2z = nx * fx, ny * fy, nz * fz
    np2 = fx // (LANES // fz)
    ry1 = up(cy + 4, 8)
    ty = up(fy + 5, 8)
    tiles = up(n2z, LANES) // LANES
    V = pltpu.VMEM
    ext0 = (bx + 16, by + 16, LANES)
    ext1 = (cx // 2 + 10, cy + 32, LANES)
    wide = max(nx, ny, nz) * 2
    dma = pltpu.SemaphoreType.DMA
    scratch = [
        V(ext0, F32), V(ext0, F32), V(ext0, F32),
        V((bx + 16, by, LANES), F32), V((bx + 16, cy, LANES), F32),
        V(ext1, F32), V(ext1, F32), V(ext1, F32),
        V((cx // 2, cy, LANES), F32),
        V((cx + 20, ry1 + fy, LANES), F32),
        V((nz, ny, nx * np2, fy, LANES), F32),
        V((tiles, n2x, n2y, LANES), F32),
        V((n2x, ty, LANES), F32), V((np2, fy, LANES), F32), V((cx + 4, ry1, LANES), F32),
        V((2 * bz, bz + LANES), BF16), V((2 * bz, bz + LANES), BF16),
        V((by + cy, 3 * (by + 16)), BF16),
        V((2 * cz, LANES), BF16), V((2 * cz, LANES), BF16),
        V((ry1 + fy, 3 * (cy + 32)), BF16),
        V((tiles * LANES, LANES), BF16), V((tiles * LANES, LANES), BF16),
        V((3 * ty, 3 * n2y), BF16),
        V((fx + 5, n2x, LANES), F32),
        V((LANES, LANES), BF16), V((ry1, 2 * up(ty, 16)), BF16),
        V((LANES, bz), BF16), V((by, 2 * up(ry1, 16)), BF16),
        dma((8,)), dma((8,)), dma((5, 2)), dma((5, 2)),
        dma((8,)), dma((8,)), dma((5, 2)), dma((5, 2)),
        dma((4, wide)), dma((3, wide)),
    ]
    return pl.pallas_call(
        functools.partial(kernel, counts, dims),
        out_shape=jax.ShapeDtypeStruct(dims, F32),
        in_specs=[pl.BlockSpec(memory_space=pltpu.SMEM), pl.BlockSpec(memory_space=pltpu.VMEM)],
        out_specs=pl.BlockSpec(memory_space=pltpu.VMEM),
        scratch_shapes=scratch,
        compiler_params=pltpu.CompilerParams(
            collective_id=0, has_side_effects=True, vmem_limit_bytes=60 * 2**20
        ),
    )(kernel_taps, charges)


def solution(mesh):
    counts = tuple(mesh.shape[a] for a in AXES)
    return jax.shard_map(
        functools.partial(per_device, counts), mesh=mesh,
        in_specs=(P("gx", "gy", "gz"), P()), out_specs=P("gx", "gy", "gz"), check_vma=False,
    )
```

profile of v0, /device:TPU:1, one launch (start us, length us, event | category | flops | bytes accessed | tf_op | source)
XLA Modules:
  0.0 73.1 jit_solution(10682144458088783918)
XLA Ops:
  0.0 70.8 %shard_map.28 = f32[32,64,128]{2,1,0:T(8,128)} custom-call(f32[5,3,17]{2,1,0:T(4,128)} %taps.1, f32[32,64,128]{2,1,0:T(8,128)} %x_ref.1), custom_call_target="tpu_custom_call" | custom-call | tf_op jit(solution)/shard_map/pallas_call | solution.py:504
  70.8 2.3 %copy.4 = f32[32,64,128]{2,1,0:T(8,128)} copy(f32[32,64,128]{2,1,0:T(8,128)} %shard_map.28) | data formatting | bytes 2097152
where the time goes:
time: 73.3 us; the launch traced here: 73.1 us
  Pallas kernels  70.8 us (97%)
  local copies, waits for them, and re-layouts  2.31 us (3%)
    pallas_call x1, Pallas kernels, per_device(): pl.pallas_call(functools.partial(kernel, counts, dims), out_shape=jax.Sha...  70.8 us
    unnamed x1, local copies, waits for them, and re-layouts  2.31 us

commit v1 on v0

--- a/solution.py
+++ b/solution.py
@@ -109,12 +109,20 @@
     zero_halo(e1, 5, 16, cx // 2, cy)
     pl.semaphore_wait(barrier, total)
 
-    def exchange(src, base, ref, wx, wy, mx, my, send, recv):
+    def exchange(src, base, ref, wx, wy, mx, my, send, recv, near, far=False):
         out = []
         for k, (a, b) in enumerate(SIDES):
-            sx = {-1: (0, wx), 0: (0, mx), 1: (mx - wx, wx)}[a]
+            if far and a == 0:
+                continue
+            rest_x = wx - near
+            if far:
+                sx = {-1: (near, rest_x), 1: (mx - wx, rest_x)}[a]
+                tx = {-1: (wx + mx + near, rest_x), 1: (0, rest_x)}[a]
+            else:
+                sx = {-1: (0, near), 0: (0, mx), 1: (mx - near, near)}[a]
+                tx = {-1: (wx + mx, near), 0: (wx, mx), 1: (wx - near, near)}[a]
+            k += len(SIDES) if far else 0
             sy = {-1: (0, wy), 0: (0, my), 1: (my - wy, wy)}[b]
-            tx = {-1: (wx + mx, wx), 0: (wx, mx), 1: (0, wx)}[a]
             ty = {-1: (wy + my, wy), 0: (wy, my), 1: (0, wy)}[b]
             copy = pltpu.make_async_remote_copy(
                 src_ref=src.at[pl.ds(base[0] + sx[0], sx[1]), pl.ds(base[1] + sy[0], sy[1]), :],
@@ -151,19 +159,22 @@
         for to, _, copy in copies:
             pl.when(to)(copy.wait_send)
 
-    def pieces(wx, wy, mx, my, direct):
+    def pieces(wx, wy, mx, my, direct, near):
         o = (wx, wy) if direct else (0, 0)
         n = (0, 0)
         return [
             (o, (wx, mx), (wy, my)),
-            (n, (0, wx), (0, my + 2 * wy)),
-            (n, (wx + mx, wx), (0, my + 2 * wy)),
+            (n, (wx - near, near), (0, my + 2 * wy)),
+            (n, (wx + mx, near), (0, my + 2 * wy)),
             (n, (wx, mx), (0, wy)),
             (n, (wx, mx), (wy + my, wy)),
+            (n, (0, wx - near), (0, my + 2 * wy)),
+            (n, (wx + mx + near, wx - near), (0, my + 2 * wy)),
         ]
 
-    xa = exchange(x_ref, (0, 0), e0, 8, 8, bx, by, sa, ra)
-    za = across(x_ref, e0, l0, r0, pieces(8, 8, bx, by, True), sza, rza)
+    xa = exchange(x_ref, (0, 0), e0, 8, 8, bx, by, sa, ra, 4)
+    xa_far = exchange(x_ref, (0, 0), e0, 8, 8, bx, by, sa, ra, 4, True)
+    za = across(x_ref, e0, l0, r0, pieces(8, 8, bx, by, True, 4), sza, rza)
     start(xa)
     start(za[:2])
     e0[pl.ds(8, bx), pl.ds(8, by), :] = x_ref[...]
@@ -185,6 +196,58 @@
     put(w0h, w0l, jnp.concatenate([k0, rz], axis=1))
     i, j = grids(by + cy, by + 16)
     stack(m0, jnp.where(i < by, pick(taps, 0, 1, j - i, i < by), cubic(j - 8 - 2 * (i - by), i >= by)), 3)
+    lane = lax.broadcasted_iota(jnp.int32, (1, LANES), 1)
+    flat = [k for k, (a, _) in enumerate(SIDES) if a == 0]
+    tilted = [k for k, (a, _) in enumerate(SIDES) if a != 0]
+    arrive([xa[k] for k in flat])
+    start(za[6:10])
+    arrive(za[:2] + za[6:10])
+
+    wide = by + 16
+    has_r, has_l = there(0, 0, 1), there(0, 0, -1)
+    mask_r, mask_l = (lane < LANES // 2) & has_r, (lane >= LANES // 2) & has_l
+    step0 = 4
+
+    def level0(c):
+        at = pl.ds(c * step0, step0)
+        own = e0[at].reshape(step0 * wide, LANES)
+        other = jnp.where(
+            mask_r, r0[at].reshape(step0 * wide, LANES),
+            jnp.where(mask_l, l0[at].reshape(step0 * wide, LANES), 0.0),
+        )
+        v = dot_right(jnp.concatenate([own, other], axis=1), (w0h, w0l))
+        for k in range(step0):
+            o = dot_left(m0, v[k * wide:(k + 1) * wide], 3)
+            y0[c * step0 + k] = o[:by, :LANES]
+            y1[c * step0 + k] = o[by:, LANES:]
+
+    pl.loop(8 // step0, (8 + bx) // step0)(level0)
+    arrive([xa[k] for k in tilted])
+    start(za[2:6])
+    arrive(za[2:6])
+    level0(4 // step0)
+    level0((8 + bx) // step0)
+
+    def restrict_x(ref, at):
+        return (
+            ref[at] + 0.5625 * (ref[at - 1] + ref[at + 1]) - 0.0625 * (ref[at - 3] + ref[at + 3])
+        )
+
+    @pl.loop(0, cx // 2)
+    def _(p):
+        a = restrict_x(y1, 8 + 4 * p)
+        b = restrict_x(y1, 10 + 4 * p)
+        t1[p] = jnp.where(lane < cz, a, pltpu.roll(b, cz, 1))
+
+    own_copy = pltpu.make_async_copy(t1, e1.at[pl.ds(5, cx // 2), pl.ds(16, cy), :], sg.at[3, 0])
+    own_copy.start()
+    own_copy.wait()
+    xb = exchange(e1, (5, 16), e1, 5, 16, cx // 2, cy, sb, rb, 2)
+    xb_far = exchange(e1, (5, 16), e1, 5, 16, cx // 2, cy, sb, rb, 2, True)
+    zb = across(e1, e1, l1, r1, pieces(5, 16, cx // 2, cy, False, 2), szb, rzb)
+    start(xb)
+    start(zb[:2])
+
     i, j = grids(2 * cz, LANES)
     pos = jnp.where(i < cz + cz // 2, i, i - 2 * cz)
     kk = j - 2
@@ -196,114 +259,14 @@
     i, j = grids(ry1 + fy, cy + 32)
     ok = (i < cy + 4) & inside(gy * cy + i - 2, ny * cy)
     stack(m1, pick(taps, 1, 1, j - 16 - (i - 2) + 8, ok) + cubic(j - 16 - 2 * (i - ry1), i >= ry1), 3)
-    def plain(axis, level, n, pad, turned):
-        i, j = grids(pad, pad)
-        d = (i - j if turned else j - i) + 8
-        return pick(taps, level, axis, d, (i < n) & (j < n))
-
-    def rest(n, pad, big, turned_r):
-        i, j = grids(*((big, pad) if turned_r else (pad, big)))
-        c, f = (j, i) if turned_r else (i, j)
-        return cubic(f - 2 * c, (c < n) & (f < 2 * n))
-
-    def operators(axis, n2, first, rows, count):
-        n3, n4 = n2 // 2, n2 // 4
-        q = up(n2, LANES)
-        i, j = grids(rows, q)
-        g = first + i
-        ok = (i < count) & inside(g, n2)
-        one = pick(taps, 2, axis, j - g + 8, ok & (j < n2))
-        pr = cubic(g - 2 * j, ok & (j < n3))
-        r23, r34 = rest(n3, q, q, False), rest(n4, q, q, False)
-        p34 = rest(n4, q, q, True)
-        two = exact(exact(pr, plain(axis, 3, n3, q, False)), r23)
-        three = exact(exact(exact(exact(pr, p34), plain(axis, 4, n4, q, False)), r34), r23)
-        return one, two, three
-
-    n2x, n2y, n2z = nx * fx, ny * fy, nz * fz
-    ez, ey, ex = fz + 5, fy + 5, fx + 5
-    tz = 40
-    row = lax.broadcasted_iota(jnp.int32, (LANES, 1), 0)
-    ops = operators(2, n2z, gz * fz - 2, tz, ez)
-    cols = jnp.concatenate(list(ops) + [jnp.zeros((LANES - 3 * tz, ops[0].shape[1]), F32)], axis=0)
-    put(w2h, w2l, cols.T)
-    ty = up(ey, 8)
-    ops = operators(1, n2y, gy * fy - 2, ty, ey)
-    stack(m2, jnp.concatenate(list(ops), axis=0)[:, :n2y], 3)
-    tx = up(ex, 8)
-    ops = operators(0, n2x, gx * fx - 2, tx, ex)
-    lane = lax.broadcasted_iota(jnp.int32, (1, LANES), 1)
-    tall = [o.T for o in ops]
-    for r in range(ex):
-        a, b, c = (o[:n2x, r:r + 1] for o in tall)
-        c2[r] = jnp.where(lane < tz, a, jnp.where(lane < 2 * tz, b, c))
-    i, j = grids(LANES, LANES)
-    src = i - jnp.where(i < tz, 0, jnp.where(i < 2 * tz, tz, 2 * tz)) - 2
-    put(pz2, None, cubic((j - 2) - 2 * src, (i < 3 * tz) & (src < fz + 3) & (j < top) & inside(gz * cz + j - 2, nz * cz)))
-    i, j = grids(ry1, up(ty, 16))
-    stack(py2, cubic((i - 2) - 2 * (j - 2), (j < ey) & (i < cy + 4) & inside(gy * cy + i - 2, ny * cy)), 2)
-    i, j = grids(LANES, bz)
-    put(pz1, None, cubic(j - 2 * (i - 2), i < top))
-    i, j = grids(by, up(ry1, 16))
-    stack(py1, cubic(i - 2 * (j - 2), j < cy + 4), 2)
-
-    arrive(xa)
-    start(za[2:])
-    arrive(za)
-
-    wide = by + 16
-    has_r, has_l = there(0, 0, 1), there(0, 0, -1)
-    mask_r, mask_l = (lane < LANES // 2) & has_r, (lane >= LANES // 2) & has_l
-    step0 = 4
-
-    @pl.loop(0, (bx + 16) // step0)
-    def _(c):
-        at = pl.ds(c * step0, step0)
-        own = e0[at].reshape(step0 * wide, LANES)
-        other = jnp.where(
-            mask_r, r0[at].reshape(step0 * wide, LANES),
-            jnp.where(mask_l, l0[at].reshape(step0 * wide, LANES), 0.0),
-        )
-        v = dot_right(jnp.concatenate([own, other], axis=1), (w0h, w0l))
-        for k in range(step0):
-            o = dot_left(m0, v[k * wide:(k + 1) * wide], 3)
-            y0[c * step0 + k] = o[:by, :LANES]
-            y1[c * step0 + k] = o[by:, LANES:]
-
-    def restrict_x(ref, at):
-        return (
-            ref[at] + 0.5625 * (ref[at - 1] + ref[at + 1]) - 0.0625 * (ref[at - 3] + ref[at + 3])
-        )
-
-    @pl.loop(0, cx // 2)
-    def _(p):
-        a = restrict_x(y1, 8 + 4 * p)
-        b = restrict_x(y1, 10 + 4 * p)
-        t1[p] = jnp.where(lane < cz, a, pltpu.roll(b, cz, 1))
-
-    own_copy = pltpu.make_async_copy(t1, e1.at[pl.ds(5, cx // 2), pl.ds(16, cy), :], sg.at[3, 0])
-    own_copy.start()
-    own_copy.wait()
-    xb = exchange(e1, (5, 16), e1, 5, 16, cx // 2, cy, sb, rb)
-    zb = across(e1, e1, l1, r1, pieces(5, 16, cx // 2, cy, False), szb, rzb)
-    start(xb)
-    start(zb[:2])
-
-    @pl.loop(0, bx)
-    def _(p):
-        acc = taps[0, 0, 0] * y0[p]
-        for t in range(1, 17):
-            acc = acc + taps[0, 0, t] * y0[p + t]
-        out_ref[p] = acc
-
-    arrive(xb)
-    start(zb[2:])
-    arrive(zb)
+
+    arrive([xb[k] for k in flat])
+    start(zb[6:10])
+    arrive(zb[:2] + zb[6:10])
 
     half = lax.rem(lane, cz) < cz // 2
 
-    @pl.loop(0, cx // 2 + 10)
-    def _(p):
+    def level1(p):
         own = e1[p]
         other = jnp.where(half & has_r, r1[p], jnp.where(jnp.logical_not(half) & has_l, l1[p], 0.0))
         even = jnp.where(lane < cz, own, pltpu.roll(other, cz, 1))
@@ -313,6 +276,13 @@
         o = dot_left(m1, jnp.concatenate([v[:h], v[h:]], axis=1), 3)
         s1[2 * p] = o[:, :LANES]
         s1[2 * p + 1] = o[:, LANES:]
+
+    pl.loop(5, 5 + cx // 2)(level1)
+    arrive([xb[k] for k in tilted])
+    start(zb[2:6])
+    arrive(zb[2:6])
+    pl.loop(3, 5)(level1)
+    pl.loop(5 + cx // 2, 7 + cx // 2)(level1)
 
     per = LANES // fz
     def restrict_1(q):
@@ -366,6 +336,71 @@
 
     ca = spread(0, nx, lambda k: g2.at[gz, gy, pl.ds(k * np2, np2)], 0)
     begin(ca)
+    start(xa_far)
+    start(xb_far)
+    def plain(axis, level, n, pad, turned):
+        i, j = grids(pad, pad)
+        d = (i - j if turned else j - i) + 8
+        return pick(taps, level, axis, d, (i < n) & (j < n))
+
+    def rest(n, pad, big, turned_r):
+        i, j = grids(*((big, pad) if turned_r else (pad, big)))
+        c, f = (j, i) if turned_r else (i, j)
+        return cubic(f - 2 * c, (c < n) & (f < 2 * n))
+
+    def operators(axis, n2, first, rows, count):
+        n3, n4 = n2 // 2, n2 // 4
+        q = up(n2, LANES)
+        i, j = grids(rows, q)
+        g = first + i
+        ok = (i < count) & inside(g, n2)
+        one = pick(taps, 2, axis, j - g + 8, ok & (j < n2))
+        pr = cubic(g - 2 * j, ok & (j < n3))
+        r23, r34 = rest(n3, q, q, False), rest(n4, q, q, False)
+        p34 = rest(n4, q, q, True)
+        two = exact(exact(pr, plain(axis, 3, n3, q, False)), r23)
+        three = exact(exact(exact(exact(pr, p34), plain(axis, 4, n4, q, False)), r34), r23)
+        return one, two, three
+
+    n2x, n2y, n2z = nx * fx, ny * fy, nz * fz
+    ez, ey, ex = fz + 5, fy + 5, fx + 5
+    tz = 40
+    ops = operators(2, n2z, gz * fz - 2, tz, ez)
+    cols = jnp.concatenate(list(ops) + [jnp.zeros((LANES - 3 * tz, ops[0].shape[1]), F32)], axis=0)
+    put(w2h, w2l, cols.T)
+    ty = up(ey, 8)
+    ops = operators(1, n2y, gy * fy - 2, ty, ey)
+    stack(m2, jnp.concatenate(list(ops), axis=0)[:, :n2y], 3)
+    tx = up(ex, 8)
+    ops = operators(0, n2x, gx * fx - 2, tx, ex)
+    tall = [o.T for o in ops]
+    for r in range(ex):
+        a, b, c = (o[:n2x, r:r + 1] for o in tall)
+        c2[r] = jnp.where(lane < tz, a, jnp.where(lane < 2 * tz, b, c))
+    i, j = grids(LANES, LANES)
+    src = i - jnp.where(i < tz, 0, jnp.where(i < 2 * tz, tz, 2 * tz)) - 2
+    put(pz2, None, cubic((j - 2) - 2 * src, (i < 3 * tz) & (src < fz + 3) & (j < top) & inside(gz * cz + j - 2, nz * cz)))
+    i, j = grids(ry1, up(ty, 16))
+    stack(py2, cubic((i - 2) - 2 * (j - 2), (j < ey) & (i < cy + 4) & inside(gy * cy + i - 2, ny * cy)), 2)
+    i, j = grids(LANES, bz)
+    put(pz1, None, cubic(j - 2 * (i - 2), i < top))
+    i, j = grids(by, up(ry1, 16))
+    stack(py1, cubic(i - 2 * (j - 2), j < cy + 4), 2)
+
+    landed(ca)
+    cb = spread(1, ny, lambda k: g2.at[gz, k], 0)
+    begin(cb)
+    arrive(xa_far)
+    start(za[10:])
+    arrive(xb_far)
+    start(zb[10:])
+    arrive(za[10:])
+    level0(0)
+    level0((12 + bx) // step0)
+    arrive(zb[10:])
+    pl.loop(0, 3)(level1)
+    pl.loop(7 + cx // 2, 10 + cx // 2)(level1)
+
     seen = lambda r: inside(gx * cx + r - 2, nx * cx).astype(F32)
 
     @pl.loop(0, cx + 4)
@@ -375,9 +410,14 @@
         for t in range(1, 17):
             acc = acc + taps[1, 0, t] * s1[p + t, rows]
         d1[p] = acc
-    landed(ca)
-    cb = spread(1, ny, lambda k: g2.at[gz, k], 0)
-    begin(cb)
+
+    @pl.loop(0, bx)
+    def _(p):
+        acc = taps[0, 0, 0] * y0[p]
+        for t in range(1, 17):
+            acc = acc + taps[0, 0, t] * y0[p + t]
+        out_ref[p] = acc
+
     landed(cb)
     cc = spread(2, nz, lambda k: g2.at[k], 0)
     begin(cc)
@@ -456,7 +496,7 @@
             0.5625 * (y0[at] + y0[at + 1]) - 0.0625 * (y0[at - 1] + y0[at + 2])
         )
 
-    for group in (xa, za, xb, zb):
+    for group in (xa, xa_far, za, xb, xb_far, zb):
         left_over(group)
     for group in (ca, cb, cc):
         for to, _, copy, _ in group:
@@ -497,8 +537,8 @@
         V((fx + 5, n2x, LANES), F32),
         V((LANES, LANES), BF16), V((ry1, 2 * up(ty, 16)), BF16),
         V((LANES, bz), BF16), V((by, 2 * up(ry1, 16)), BF16),
-        dma((8,)), dma((8,)), dma((5, 2)), dma((5, 2)),
-        dma((8,)), dma((8,)), dma((5, 2)), dma((5, 2)),
+        dma((16,)), dma((16,)), dma((7, 2)), dma((7, 2)),
+        dma((16,)), dma((16,)), dma((7, 2)), dma((7, 2)),
         dma((4, wide)), dma((3, wide)),
     ]
     return pl.pallas_call(

time: 73.3 us -> 64.6 us (0.88)
  Pallas kernels: 70.8 us -> 61.7 us
    pallas_call x1, Pallas kernels: 70.8 us -> 61.7 us  [per_device(): pl.pallas_call(functools.partial(kernel, counts, dims), out_shape=jax.Sha...]
where the time goes in v1:
time: 64.6 us; the launch traced here: 64 us
  Pallas kernels  61.7 us (96%)
  local copies, waits for them, and re-layouts  2.31 us (4%)
    pallas_call x1, Pallas kernels, per_device(): pl.pallas_call(functools.partial(kernel, counts, dims), out_shape=jax.Sha...  61.7 us
    unnamed x1, local copies, waits for them, and re-layouts  2.31 us

profile of v1, /device:TPU:1, one launch (start us, length us, event | category | flops | bytes accessed | tf_op | source)
XLA Modules:
  0.0 64.0 jit_solution(10184174212467308997)
XLA Ops:
  0.0 61.7 %shard_map.28 = f32[32,64,128]{2,1,0:T(8,128)} custom-call(f32[5,3,17]{2,1,0:T(4,128)} %taps.1, f32[32,64,128]{2,1,0:T(8,128)} %x_ref.1), custom_call_target="tpu_custom_call" | custom-call | tf_op jit(solution)/shard_map/pallas_call | solution.py:544
  61.7 2.3 %copy.4 = f32[32,64,128]{2,1,0:T(8,128)} copy(f32[32,64,128]{2,1,0:T(8,128)} %shard_map.28) | data formatting | bytes 2097152
